TPU v7x, 32 devices: a whole 2x2x4 slice. The times are simulated.
32 devices in a mesh: seq: 8 (over z, core), tp: 4 (over y, x).
Axes of the slice: x: 2, y: 2, z: 4, core: 2. Of those that a mesh axis runs over, the one named last changes fastest.
Arguments:
- tokens: bfloat16 [2048, 4608], P('seq', 'tp'), may hold values from -6 to 6
- attention_gain: float32 [4608], replicated, may hold values from 0.25 to 1.75
- query_weight: bfloat16 [4608, 4096], P(None, 'tp'), may hold values from -0.09375 to 0.09375
- key_weight: bfloat16 [4608, 2048], P(None, 'tp'), may hold values from -0.09375 to 0.09375
- value_weight: bfloat16 [4608, 2048], P(None, 'tp'), may hold values from -0.09375 to 0.09375
- output_weight: bfloat16 [4096, 4608], P('tp'), may hold values from -0.09375 to 0.09375
- post_gain: float32 [4608], replicated, may hold values from 0.25 to 1.75
- local_gain: float32 [4608], replicated, may hold values from 0.25 to 1.75
- local_query_weight: bfloat16 [4608, 4096], P(None, 'tp'), may hold values from -0.09375 to 0.09375
- local_key_weight: bfloat16 [4608, 2048], P(None, 'tp'), may hold values from -0.09375 to 0.09375
- local_value_weight: bfloat16 [4608, 2048], P(None, 'tp'), may hold values from -0.09375 to 0.09375
Outputs:
- hidden: bfloat16 [2048, 4608], P('seq', 'tp')
- local_heads: bfloat16 [2048, 4096], P('seq', 'tp')
All inputs are finite; a program needn't handle non-finite values.
Results may differ from a plain program's by a relative error of at most 0.02.
Values may be sent and summed in bfloat16 or wider, within the bound.
A program may use at most 128 MiB of HBM per device.

v0:
```python
import jax
import jax.numpy as jnp
from jax import lax
from jax.sharding import PartitionSpec as P

D = 4608
HEADS = 32
HEAD_DIM = 128
SOFT_CAP = 50.0
NORM_EPS = 1e-06


def passed_along(value, axis, steps):
    count = lax.axis_size(axis)
    leading, last = (max(0, -steps), min(count, count - steps))
    return lax.ppermute(value, axis, [(source, source + steps) for source in range(leading, last)])


def rms_scaled(values, weights):
    widened = values.astype(jnp.float32)
    factor = lax.rsqrt(jnp.mean(widened * widened, axis=-1, keepdims=True) + NORM_EPS)
    return widened * factor * weights


def rotate(vectors, places):
    head_size = vectors.shape[-1]
    halfway = head_size // 2
    exponents = jnp.arange(halfway, dtype=jnp.float32) * (2.0 / head_size)
    frequency = jnp.power(jnp.float32(10000.0), -exponents)
    angles = places.astype(jnp.float32)[:, None] * frequency[None, :]
    cosine_part = jnp.cos(angles)[:, None, :]
    sine_part = jnp.sin(angles)[:, None, :]
    first_half = vectors[..., :halfway]
    second_half = vectors[..., halfway:]
    return jnp.concatenate(
        [
            first_half * cosine_part - second_half * sine_part,
            second_half * cosine_part + first_half * sine_part,
        ],
        axis=-1,
    )


def project_heads(normed, weight_query, weight_key, weight_value, places):
    row_count = normed.shape[0]
    queries = jnp.dot(normed, weight_query, preferred_element_type=jnp.float32).reshape(
        row_count, -1, HEAD_DIM
    )
    key_heads = jnp.dot(normed, weight_key, preferred_element_type=jnp.float32).reshape(
        row_count, -1, HEAD_DIM
    )
    value_heads = jnp.dot(normed, weight_value, preferred_element_type=jnp.float32).reshape(
        row_count, -1, HEAD_DIM
    )
    return (
        rotate(queries, places).astype(jnp.bfloat16),
        rotate(key_heads, places).astype(jnp.bfloat16),
        value_heads.astype(jnp.bfloat16),
    )


def empty_carry(queries, kv_heads):
    row_count = queries.shape[0]
    groups = queries.shape[1] // kv_heads
    return (
        jnp.zeros((row_count, kv_heads, groups, HEAD_DIM), jnp.float32),
        jnp.zeros((kv_heads, groups, row_count), jnp.float32),
    )


def attend_block(queries, query_places, key_block, value_block, key_places, window_size):
    kv_heads = key_block.shape[1]
    groups = queries.shape[1] // kv_heads
    grouped = queries.reshape(queries.shape[0], kv_heads, groups, queries.shape[2])
    scale = float(D // HEADS) ** (-0.5)
    scores = (
        jnp.einsum("qhrd,khd->hrqk", grouped, key_block, preferred_element_type=jnp.float32) * scale
    )
    scores = SOFT_CAP * jnp.tanh(scores / SOFT_CAP)
    offset = query_places[:, None] - key_places[None, :]
    allowed = (offset >= 0) & (key_places >= 0)[None, :]
    if window_size is not None:
        allowed = allowed & (offset < window_size)
    weights = jnp.where(allowed[None, None], jnp.exp(scores), jnp.float32(0.0))
    denominator = jnp.sum(weights, axis=-1)
    numerator = jnp.einsum(
        "hrqk,khd->qhrd",
        weights.astype(jnp.bfloat16),
        value_block,
        preferred_element_type=jnp.float32,
    )
    return (numerator, denominator)


def finish_heads(running):
    numerator, denominator = running
    averaged = numerator / jnp.transpose(denominator, (2, 0, 1))[..., None]
    return averaged.astype(jnp.bfloat16).reshape(numerator.shape[0], -1)


def visit_one(partial_sum, query_set, key_block, value_block, key_places, needed):

    def compute(current):
        return attend_block(query_set[0], query_set[1], key_block, value_block, key_places, None)

    return lax.cond(needed, compute, lambda current: current, partial_sum)


def causal_sets(query_sets, key_heads, value_heads):
    kv_heads = key_heads.shape[1]
    initial = tuple((empty_carry(query_set[0], kv_heads) for query_set in query_sets))
    latest = tuple((jnp.max(query_set[1]) for query_set in query_sets))
    first_row = jnp.int32(0)
    key_block = lax.all_gather(key_heads, "seq", axis=0, tiled=True)
    value_block = lax.all_gather(value_heads, "seq", axis=0, tiled=True)
    key_places = lax.iota(jnp.int32, key_block.shape[0])
    updated = []
    for query_set, visit_partial_sum, newest in zip(query_sets, initial, latest):
        updated.append(
            visit_one(
                visit_partial_sum,
                query_set,
                key_block,
                value_block,
                key_places,
                first_row <= newest,
            )
        )
    totals = tuple(updated)
    return [finish_heads(partial_sum) for partial_sum in totals]


def local(
    tokens,
    attention_gain,
    query_weight,
    key_weight,
    value_weight,
    output_weight,
    post_gain,
    local_gain,
    local_query_weight,
    local_key_weight,
    local_value_weight,
):
    row_count = tokens.shape[0]
    column_count = tokens.shape[1]
    section_index = lax.axis_index("seq")
    places = section_index * row_count + lax.iota(jnp.int32, row_count)
    full_rows = lax.all_gather(tokens, "tp", axis=1, tiled=True)
    normed = rms_scaled(full_rows, attention_gain).astype(jnp.bfloat16)
    queries, key_heads, value_heads = project_heads(
        normed, query_weight, key_weight, value_weight, places
    )
    attended = causal_sets([(queries, places)], key_heads, value_heads)[0]
    summed = lax.psum(
        jnp.dot(attended, output_weight, preferred_element_type=jnp.float32).astype(jnp.bfloat16),
        "tp",
    ).astype(jnp.float32)
    whole_hidden = (full_rows.astype(jnp.float32) + rms_scaled(summed, post_gain)).astype(
        jnp.bfloat16
    )
    hidden = lax.dynamic_slice_in_dim(
        whole_hidden, lax.axis_index("tp") * column_count, column_count, 1
    )
    local_normed = rms_scaled(whole_hidden, local_gain).astype(jnp.bfloat16)
    local_queries, local_keys, local_values = project_heads(
        local_normed, local_query_weight, local_key_weight, local_value_weight, places
    )
    window_size = row_count // 2
    tails = jnp.stack(
        [local_keys[row_count - window_size :], local_values[row_count - window_size :]]
    )
    earlier = passed_along(tails, "seq", 1)
    key_block = jnp.concatenate([earlier[0], local_keys], axis=0)
    value_block = jnp.concatenate([earlier[1], local_values], axis=0)
    key_places = (
        section_index * row_count - window_size + lax.iota(jnp.int32, window_size + row_count)
    )
    result = attend_block(local_queries, places, key_block, value_block, key_places, window_size)
    local_heads = finish_heads(result)
    return (hidden, local_heads)


def solution(mesh):
    in_specs = (
        P("seq", "tp"),
        P(),
        P(None, "tp"),
        P(None, "tp"),
        P(None, "tp"),
        P("tp", None),
        P(),
        P(),
        P(None, "tp"),
        P(None, "tp"),
        P(None, "tp"),
    )
    out_specs = (P("seq", "tp"), P("seq", "tp"))
    return jax.shard_map(local, mesh=mesh, in_specs=in_specs, out_specs=out_specs, check_vma=False)
```

profile of v0, /device:TPU:1, one launch (start us, length us, event | category | flops | bytes accessed | tf_op | source)
XLA Modules:
  0.0 260.0 jit_solution(231217193242092318)
XLA Ops:
  9.2 39.9 %all-gather.4.cloned.1.call-done = bf16[256,4608]{1,0:T(8,128)(2,1)} async-done(((bf16[256,1152]{1,0:T(8,128)(2,1)}), bf16[256,4608]{1,0:T(8,128)(2,1)}) %all-gather.4.cloned.1.call-update) | async-done | bytes 2359312 | tf_op jit(solution)/shard_map/all_gather | solution.py:150
  49.1 2.2 fusion.22
  51.3 5.3 %fusion.58 = f32[256,512]{1,0:T(8,128)} fusion(bf16[4608,512]{1,0:T(8,128)(2,1)} %param.16, bf16[256,4608]{1,0:T(8,128)(2,1)} %all-gather.4.cloned.1.call-done, f32[4608]{0:T(1024)} %param.14, f32[256]{0:T(256)S(1)} %add_rsqrt_fusion.2), kind=kOutput, calls=%fused_computation.94 | convolution fusion | flops 1212678144 | bytes 7621632 | tf_op jit(solution)/shard_map/dot_general | solution.py:49
  56.6 1.4 reshape.222
  58.5 0.9 pad_maximum_fusion.1
  59.4 3.8 %fusion.34 = bf16[32,4,8,128]{3,2,1,0:T(8,128)(2,1)S(1)} fusion(bf16[4608,512]{1,0:T(8,128)(2,1)} %param.17, bf16[256,4608]{1,0:T(8,128)(2,1)S(1)} %copy-done, f32[4608]{0:T(1024)S(1)} %copy-done.15, f32[256]{0:T(256)S(1)} %add_rsqrt_fusion.2), kind=kOutput, calls=%fused_computation.42 | convolution fusion | flops 1212809216 | bytes 7359488 | tf_op jit(solution)/shard_map/dot_general | solution.py:52
  65.2 5.6 %convolution_bitcast_fusion.1 = f32[32,8,8,128]{3,1,2,0:T(8,128)S(1)} fusion(bf16[4608,1024]{1,0:T(8,128)(2,1)} %param.15, bf16[256,4608]{1,0:T(8,128)(2,1)S(1)} %copy-done, f32[4608]{0:T(1024)S(1)} %copy-done.15, f32[256]{0:T(256)S(1)} %add_rsqrt_fusion.2), kind=kOutput, calls=%fused_computation.38 | convolution fusion | flops 2420637696 | bytes 12864512 | tf_op jit(solution)/shard_map/dot_general | solution.py:46
  71.8 1.1 pad_maximum_fusion
  72.8 16.4 %all-gather.6.cloned.1.call-done = bf16[2048,4,128]{2,0,1:T(8,128)(2,1)} async-done(((bf16[256,4,128]{2,0,1:T(8,128)(2,1)}), bf16[2048,4,128]{2,0,1:T(8,128)(2,1)}) %all-gather.6.cloned.1.call-update) | async-done | bytes 2097168 | tf_op jit(solution)/shard_map/all_gather | solution.py:114
  89.2 30.2 %all-gather.8.cloned.1.call-done = bf16[2048,4,128]{2,0,1:T(8,128)(2,1)} async-done(((bf16[256,4,128]{2,0,1:T(8,128)(2,1)}), bf16[2048,4,128]{2,0,1:T(8,128)(2,1)}) %all-gather.8.cloned.1.call-update) | async-done | bytes 2097168 | tf_op jit(solution)/shard_map/all_gather | solution.py:115
  119.4 17.3 %conditional.1 = (f32[4,2,256]{2,1,0:T(2,128)S(1)}, f32[256,4,2,128]{0,3,2,1:T(8,128)S(1)}) conditional(s32[]{:T(128)} %convert_element_type.65, () %tuple.16, (s32[256]{0:T(256)}, s32[2048]{0:T(1024)S(1)}, s32[2048]{0:T(1024)S(1)}, bf16[256,8,128]{2,0,1:T(8,128)(2,1)}, bf16[2048,4,128]{2,0,1:T(8,128)(2,1)}, ...), branch_computations={%region_2.0_spmd, %region_3.5_spmd} | conditional | flops 2182610944 | bytes 51409964 | solution.py:106
  119.4 2.2 fusion.8
  121.6 6.8 %fusion = (f32[4,2,256]{2,1,0:T(2,128)S(1)}, f32[4,2048,256,2]{2,1,3,0:T(8,128)S(1)}) fusion(pred[256,2048]{0,1:T(8,128)(4,1)S(1)} %fusion.8, bf16[256,4,2,128]{3,0,2,1:T(8,128)(2,1)} %bitcast.90, bf16[2048,4,128]{2,0,1:T(8,128)(2,1)} %get-tuple-element.14), kind=kOutput, calls=%fused_computation.1 | convolution fusion | flops 1090516992 | bytes 19931136 | tf_op jit(solution)/shard_map/cond/branch_1_fun/qhrd,khd->hrqk/dot_general | solution.py:77
  128.4 6.5 %fusion.9 = f32[256,4,2,128]{3,0,2,1:T(8,128)} fusion(bf16[2048,4,128]{2,0,1:T(8,128)(2,1)S(1)} %copy-done.14, f32[4,2048,256,2]{2,1,3,0:T(8,128)S(1)} %get-tuple-element.31, pred[256,2048]{0,1:T(8,128)(4,1)S(1)} %fusion.8), kind=kOutput, calls=%fused_computation.10 | convolution fusion | flops 1090519040 | bytes 20447232 | tf_op jit(solution)/shard_map/cond/branch_1_fun/hrqk,khd->qhrd/dot_general | solution.py:86
  134.9 1.6 copy.52
  136.8 7.6 %convolution_convert_fusion = bf16[256,4608]{1,0:T(8,128)(2,1)} fusion(bf16[256,1024]{0,1:T(8,128)(2,1)S(1)} %bitcast.88, bf16[1024,4608]{1,0:T(8,128)(2,1)} %param.18), kind=kOutput, calls=%fused_computation.18 | convolution fusion | flops 2417098752 | bytes 12320768 | tf_op jit(solution)/shard_map/dot_general | solution.py:157
  144.5 0.9 fusion.48
  145.4 71.9 %all-reduce.2.cloned.1.call-done = bf16[256,4608]{1,0:T(8,128)(2,1)} async-done(((bf16[256,4608]{1,0:T(8,128)(2,1)}), bf16[256,4608]{1,0:T(8,128)(2,1)}) %all-reduce.2.cloned.1.call-update) | async-done | bytes 2359312 | tf_op jit(solution)/shard_map/psum | solution.py:156
  217.3 2.2 fusion.17
  219.6 3.2 %fusion.19 = (f32[256]{0:T(256)S(1)}, bf16[256,4608]{1,0:T(8,128)(2,1)S(1)}) fusion(f32[4608]{0:T(1024)S(1)} %copy-done.12, f32[256]{0:T(256)S(1)} %add_rsqrt_fusion.1, bf16[256,4608]{1,0:T(8,128)(2,1)} %all-reduce.2.cloned.1.call-done, bf16[256,4608]{1,0:T(8,128)(2,1)S(1)} %copy-done), kind=kLoop, calls=%fused_computation.25 | loop fusion | flops 10616576 | bytes 7098368 | tf_op jit(solution)/shard_map/reduce_sum | solution.py:21
  222.8 6.1 %convolution_bitcast_fusion = f32[32,8,8,128]{3,1,2,0:T(8,128)S(1)} fusion(bf16[4608,1024]{1,0:T(8,128)(2,1)} %param.21, bf16[256,4608]{1,0:T(8,128)(2,1)S(1)} %get-tuple-element.29, f32[4608]{0:T(1024)S(1)} %copy-done.16, f32[256]{0:T(256)S(1)} %add_rsqrt_fusion), kind=kOutput, calls=%fused_computation.37 | convolution fusion | flops 2420637696 | bytes 12864512 | tf_op jit(solution)/shard_map/dot_general | solution.py:46
  229.6 1.4 fusion.63
  231.2 1.1 fusion.68
  232.3 4.5 %convolution_convert_fusion.1 = bf16[256,512]{1,0:T(8,128)(2,1)S(1)} fusion(bf16[4608,512]{1,0:T(8,128)(2,1)} %param.23, bf16[256,4608]{1,0:T(8,128)(2,1)} %copy-done.1, f32[4608]{0:T(1024)S(1)} %copy-done.17, f32[256]{0:T(256)S(1)} %add_rsqrt_fusion), kind=kOutput, calls=%fused_computation.40 | convolution fusion | flops 1212809216 | bytes 7359488 | tf_op jit(solution)/shard_map/dot_general | solution.py:52
  238.2 0.9 stack.10
  240.2 0.8 pad_maximum_fusion.2
  241.0 4.0 %collective-permute-start = (bf16[2,128,4,128]{3,1,2,0:T(8,128)(2,1)}, bf16[2,128,4,128]{3,1,2,0:T(8,128)(2,1)S(1)}, u32[]{:S(2)}, u32[]{:S(2)}) collective-permute-start(bf16[2,128,4,128]{3,1,2,0:T(8,128)(2,1)} %pad_maximum_fusion.2), channel_id=1, source_target_pairs={{0,4},{4,8},{8,12},{12,16},{16,20},{20,24},{24,28},{1,5},{5,9},{9,... | collective-permute-start | bytes 786440 | tf_op jit(solution)/shard_map/ppermute | solution.py:16
  245.0 1.4 subtract_convert_fusion
  246.5 1.9 constant_dynamic-slice_fusion
  248.8 2.6 fusion.26
  251.3 1.1 divide_convert_fusion
  252.5 1.0 copy.43
  (78 shorter events, 8.6 us)
Async XLA Ops:
  7.2 41.9 %all-gather.4.cloned.1.call-start = ((), (), s32[]{:S(2)}) async-start(), calls=%async_computation | async-start | bytes 2949120 | tf_op jit(solution)/shard_map/all_gather | solution.py:150
  7.9 81.3 %all-gather.6.cloned.1.call-start = ((), (), s32[]{:S(2)}) async-start(), calls=%async_computation.1 | async-start | bytes 2359296 | tf_op jit(solution)/shard_map/all_gather | solution.py:114
  9.2 62.1 %copy-start.2 = (f32[256,64]{1,0:T(8,128)}, f32[256,64]{1,0:T(8,128)S(1)}, u32[]{:S(2)}) copy-start(f32[256,64]{1,0:T(8,128)S(1)} %get-tuple-element.51) | copy-start | bytes 196612
  56.6 2.8 %copy-start = (bf16[256,4608]{1,0:T(8,128)(2,1)S(1)}, bf16[256,4608]{1,0:T(8,128)(2,1)}, u32[]{:S(2)}) copy-start(bf16[256,4608]{1,0:T(8,128)(2,1)} %all-gather.4.cloned.1.call-done) | copy-start | bytes 7077892
  56.6 2.8 %copy-start.15 = (f32[4608]{0:T(1024)S(1)}, f32[4608]{0:T(1024)}, u32[]{:S(2)}) copy-start(f32[4608]{0:T(1024)} %param.14) | copy-start | bytes 55300
  59.3 60.1 %all-gather.8.cloned.1.call-start = ((), (), s32[]{:S(2)}) async-start(), calls=%async_computation.2 | async-start | bytes 2359296 | tf_op jit(solution)/shard_map/all_gather | solution.py:115
  64.0 153.3 %all-reduce.2.cloned.1.call-start = ((), (), s32[]{:S(2)}) async-start(), calls=%async_computation.3 | async-start | bytes 4718592 | tf_op jit(solution)/shard_map/psum | solution.py:156
  121.6 6.8 %copy-start.14 = (bf16[2048,4,128]{2,0,1:T(8,128)(2,1)S(1)}, bf16[2048,4,128]{2,0,1:T(8,128)(2,1)}, u32[]{:S(2)}) copy-start(bf16[2048,4,128]{2,0,1:T(8,128)(2,1)} %get-tuple-element.16) | copy-start | bytes 6291460 | tf_op jit(solution)/shard_map/cond
  136.8 7.7 %copy-start.13 = (s32[256]{0:T(256)S(1)}, s32[256]{0:T(256)}, u32[]{:S(2)}) copy-start(s32[256]{0:T(256)} %iota_add_fusion.1) | copy-start | bytes 3076
  144.4 75.1 %copy-start.12 = (f32[4608]{0:T(1024)S(1)}, f32[4608]{0:T(1024)}, u32[]{:S(2)}) copy-start(f32[4608]{0:T(1024)} %param.19) | copy-start | bytes 55300
  145.4 77.4 %copy-start.16 = (f32[4608]{0:T(1024)S(1)}, f32[4608]{0:T(1024)}, u32[]{:S(2)}) copy-start(f32[4608]{0:T(1024)} %param.20) | copy-start | bytes 55300
  219.5 10.0 %slice-start = ((s8[4718592]{0:T(1024)(128)(4,1)}), s8[4194304]{0:T(1024)(128)(4,1)S(1)}, s32[]{:S(2)}) async-start(s8[4718592]{0:T(1024)(128)(4,1)} %bitcast.96), calls=%async_computation.4 | async-start | bytes 8388608
  222.8 6.7 %copy-start.1 = (bf16[256,4608]{1,0:T(8,128)(2,1)}, bf16[256,4608]{1,0:T(8,128)(2,1)S(1)}, u32[]{:S(2)}) copy-start(bf16[256,4608]{1,0:T(8,128)(2,1)S(1)} %get-tuple-element.29) | copy-start | bytes 7077892
  222.8 6.7 %slice-start.1 = ((s8[4718592]{0:T(1024)(128)(4,1)}), s8[524288]{0:T(1024)(128)(4,1)S(1)}, s32[]{:S(2)}) async-start(s8[4718592]{0:T(1024)(128)(4,1)} %bitcast.96), calls=%async_computation.5 | async-start | bytes 1048576
  229.6 2.8 %copy-start.17 = (f32[4608]{0:T(1024)S(1)}, f32[4608]{0:T(1024)}, u32[]{:S(2)}) copy-start(f32[4608]{0:T(1024)} %param.20) | copy-start | bytes 55300
  232.3 6.9 %copy-start.3 = (f32[256,64]{1,0:T(8,128)S(1)}, f32[256,64]{1,0:T(8,128)}, u32[]{:S(2)}) copy-start(f32[256,64]{1,0:T(8,128)} %copy-done.2) | copy-start | bytes 196612
  232.3 6.9 %copy-start.4 = (f32[256,4,64]{2,1,0:T(4,128)S(1)}, f32[256,4,64]{2,1,0:T(4,128)}, u32[]{:S(2)}) copy-start(f32[256,4,64]{2,1,0:T(4,128)} %get-tuple-element.45) | copy-start | bytes 786436
  236.9 0.7 copy-start.9
  239.4 0.7 copy-start.5
  239.4 0.8 copy-start.7
  239.4 7.0 %copy-start.10 = (bf16[256,512]{1,0:T(8,128)(2,1)S(1)}, bf16[256,512]{1,0:T(8,128)(2,1)}, u32[]{:S(2)}) copy-start(bf16[256,512]{1,0:T(8,128)(2,1)} %copy-done.9) | copy-start | bytes 786436
  240.2 8.5 %copy-start.6 = (bf16[256,4,64]{2,0,1:T(8,128)(2,1)S(1)}, bf16[256,4,64]{2,0,1:T(8,128)(2,1)}, u32[]{:S(2)}) copy-start(bf16[256,4,64]{2,0,1:T(8,128)(2,1)} %copy-done.5) | copy-start | bytes 393220
  241.0 7.8 %copy-start.8 = (bf16[256,4,64]{2,0,1:T(8,128)(2,1)S(1)}, bf16[256,4,64]{2,0,1:T(8,128)(2,1)}, u32[]{:S(2)}) copy-start(bf16[256,4,64]{2,0,1:T(8,128)(2,1)} %copy-done.7) | copy-start | bytes 393220
  241.0 7.8 %copy-start.11 = (pred[256,384]{0,1:T(8,128)(4,1)S(1)}, pred[256,384]{0,1:T(8,128)(4,1)}, u32[]{:S(2)}) copy-start(pred[256,384]{0,1:T(8,128)(4,1)} %fusion.48) | copy-start | bytes 294916
  241.0 7.6 %collective-permute-start = (bf16[2,128,4,128]{3,1,2,0:T(8,128)(2,1)}, bf16[2,128,4,128]{3,1,2,0:T(8,128)(2,1)S(1)}, u32[]{:S(2)}, u32[]{:S(2)}) collective-permute-start(bf16[2,128,4,128]{3,1,2,0:T(8,128)(2,1)} %pad_maximum_fusion.2), channel_id=1, source_target_pairs={{0,4},{4,8},{8,12},{12,16},{16,20},{20,24},{24,28},{1,5},{5,9},{9,... | collective-permute-start | bytes 786440 | tf_op jit(solution)/shard_map/ppermute | solution.py:16
Sparse Core Ops, SparseCore 0:
  9.8 39.2 all-gather.3
  59.5 29.7 all-gather.5
  90.8 28.5 all-gather.7
  144.6 72.6 all-reduce.1
where the time goes:
time: 260 us
  waiting for transfers between devices  159 us (61%)
  matrix products  51.3 us (20%)
  other arithmetic  17.5 us (7%)
  between operations  14.8 us (6%)
  local copies, waits for them, and re-layouts  12.7 us (5%)
  starting transfers between devices  4.14 us (2%)
    psum x1, waiting for transfers between devices, local(): lax.psum(jnp.dot(attended, output_weight, preferred_element_type=jnp.floa...  71.9 us
    all_gather x1, waiting for transfers between devices, local(): full_rows = lax.all_gather(tokens, 'tp', axis=1, tiled=True)  39.9 us
    all_gather x1, waiting for transfers between devices, causal_sets(): value_block = lax.all_gather(value_heads, 'seq', axis=0, tiled=True)  30.2 us
    all_gather x1, waiting for transfers between devices, causal_sets(): key_block = lax.all_gather(key_heads, 'seq', axis=0, tiled=True)  16.4 us
    dot_general x2, matrix products, project_heads(): jnp.dot(normed, weight_query, preferred_element_type=jnp.float32)  11.7 us
    dot_general x2, matrix products, attend_block(): jnp.einsum('qhrd,khd->hrqk', grouped, key_block, preferred_element_type=j...  9.32 us
    dot_general x2, matrix products, project_heads(): jnp.dot(normed, weight_value, preferred_element_type=jnp.float32)  8.31 us
    dot_general x2, matrix products, attend_block(): jnp.einsum('hrqk,khd->qhrd', weights.astype(jnp.bfloat16), value_block, p...  7.66 us
  transfers between devices with their start and end apart: 5, of which 5 were waited for; matrix products, arithmetic and copies ran while one was open for 7% of the time, Pallas kernels for 0%

commit v1 on v0

--- a/solution.py
+++ b/solution.py
@@ -153,9 +153,14 @@
         normed, query_weight, key_weight, value_weight, places
     )
     attended = causal_sets([(queries, places)], key_heads, value_heads)[0]
-    summed = lax.psum(
-        jnp.dot(attended, output_weight, preferred_element_type=jnp.float32).astype(jnp.bfloat16),
-        "tp",
+    summed = jnp.sum(
+        lax.all_gather(
+            jnp.dot(attended, output_weight, preferred_element_type=jnp.float32).astype(
+                jnp.bfloat16
+            ),
+            "tp",
+        ),
+        axis=0,
     ).astype(jnp.float32)
     whole_hidden = (full_rows.astype(jnp.float32) + rms_scaled(summed, post_gain)).astype(
         jnp.bfloat16

time: 260 us -> 287 us (1.10)
  waiting for transfers between devices: 159 us -> 184 us
  other arithmetic: 17.5 us -> 20.6 us
    all_gather x0 -> x1, waiting for transfers between devices: none -> 95 us  [local(): lax.all_gather(jnp.dot(attended, output_weight, preferred_element_type=jn...]
    psum x1 -> x0, waiting for transfers between devices: 71.9 us -> none  [local(): lax.psum(jnp.dot(attended, output_weight, preferred_element_type=jnp.floa...]
    reduce_sum x0 -> x1, other arithmetic: none -> 6.49 us  [local(): jnp.sum(lax.all_gather(jnp.dot(attended, output_weight, preferred_element...]
  transfers between devices with their start and end apart: 5 -> 5, of which waited for: 5 -> 4; matrix products, arithmetic and copies ran while one was open for 7% -> 6% of each run, Pallas kernels for 0% -> 0%
where the time goes in v1:
time: 287 us; the launch traced here: 286 us
  waiting for transfers between devices  184 us (64%)
  matrix products  51 us (18%)
  other arithmetic  20.6 us (7%)
  between operations  14.8 us (5%)
  local copies, waits for them, and re-layouts  11.2 us (4%)
  starting transfers between devices  4.23 us (1%)
    all_gather x1, waiting for transfers between devices, local(): lax.all_gather(jnp.dot(attended, output_weight, preferred_element_type=jn...  95 us
    all_gather x1, waiting for transfers between devices, local(): full_rows = lax.all_gather(tokens, 'tp', axis=1, tiled=True)  39.9 us
    all_gather x1, waiting for transfers between devices, causal_sets(): value_block = lax.all_gather(value_heads, 'seq', axis=0, tiled=True)  30.8 us
    all_gather x1, waiting for transfers between devices, causal_sets(): key_block = lax.all_gather(key_heads, 'seq', axis=0, tiled=True)  17.8 us
    dot_general x2, matrix products, project_heads(): jnp.dot(normed, weight_query, preferred_element_type=jnp.float32)  11.6 us
    dot_general x2, matrix products, attend_block(): jnp.einsum('qhrd,khd->hrqk', grouped, key_block, preferred_element_type=j...  9.16 us
    dot_general x2, matrix products, project_heads(): jnp.dot(normed, weight_value, preferred_element_type=jnp.float32)  8.3 us
    dot_general x1, matrix products, local(): jnp.dot(attended, output_weight, preferred_element_type=jnp.float32)  7.6 us
  transfers between devices with their start and end apart: 5, of which 4 were waited for; matrix products, arithmetic and copies ran while one was open for 6% of the time, Pallas kernels for 0%

profile of v1, /device:TPU:1, one launch (start us, length us, event | category | flops | bytes accessed | tf_op | source)
XLA Modules:
  0.0 286.3 jit_solution(17981664426763814852)
XLA Ops:
  9.2 39.9 %all-gather.6.cloned.1.call-done = bf16[256,4608]{1,0:T(8,128)(2,1)} async-done(((bf16[256,1152]{1,0:T(8,128)(2,1)}), bf16[256,4608]{1,0:T(8,128)(2,1)}) %all-gather.6.cloned.1.call-update) | async-done | bytes 2359312 | tf_op jit(solution)/shard_map/all_gather | solution.py:150
  49.1 2.2 fusion.22
  51.3 5.3 %fusion.58 = f32[256,512]{1,0:T(8,128)} fusion(bf16[4608,512]{1,0:T(8,128)(2,1)} %param.16, bf16[256,4608]{1,0:T(8,128)(2,1)} %all-gather.6.cloned.1.call-done, f32[4608]{0:T(1024)} %param.14, f32[256]{0:T(256)S(1)} %add_rsqrt_fusion.2), kind=kOutput, calls=%fused_computation.94 | convolution fusion | flops 1212678144 | bytes 7621632 | tf_op jit(solution)/shard_map/dot_general | solution.py:49
  56.6 1.4 reshape.222
  58.5 0.9 pad_maximum_fusion.1
  59.4 3.8 %fusion.34 = bf16[32,4,8,128]{3,2,1,0:T(8,128)(2,1)S(1)} fusion(bf16[4608,512]{1,0:T(8,128)(2,1)} %param.17, bf16[256,4608]{1,0:T(8,128)(2,1)S(1)} %copy-done, f32[4608]{0:T(1024)S(1)} %copy-done.7, f32[256]{0:T(256)S(1)} %add_rsqrt_fusion.2), kind=kOutput, calls=%fused_computation.42 | convolution fusion | flops 1212809216 | bytes 7359488 | tf_op jit(solution)/shard_map/dot_general | solution.py:52
  63.2 0.7 copy.81
  64.7 5.5 %convolution_bitcast_fusion.1 = f32[32,8,8,128]{3,1,2,0:T(8,128)S(1)} fusion(bf16[4608,1024]{1,0:T(8,128)(2,1)} %param.15, bf16[256,4608]{1,0:T(8,128)(2,1)S(1)} %copy-done, f32[4608]{0:T(1024)S(1)} %copy-done.7, f32[256]{0:T(256)S(1)} %add_rsqrt_fusion.2), kind=kOutput, calls=%fused_computation.38 | convolution fusion | flops 2420637696 | bytes 12864512 | tf_op jit(solution)/shard_map/dot_general | solution.py:46
  71.4 17.8 %all-gather.8.cloned.1.call-done = bf16[2048,4,128]{2,0,1:T(8,128)(2,1)} async-done(((bf16[256,4,128]{2,0,1:T(8,128)(2,1)}), bf16[2048,4,128]{2,0,1:T(8,128)(2,1)}) %all-gather.8.cloned.1.call-update) | async-done | bytes 2097168 | tf_op jit(solution)/shard_map/all_gather | solution.py:114
  89.2 30.8 %all-gather.10.cloned.1.call-done = bf16[2048,4,128]{2,0,1:T(8,128)(2,1)} async-done(((bf16[256,4,128]{2,0,1:T(8,128)(2,1)}), bf16[2048,4,128]{2,0,1:T(8,128)(2,1)}) %all-gather.10.cloned.1.call-update) | async-done | bytes 2097168 | tf_op jit(solution)/shard_map/all_gather | solution.py:115
  120.0 14.4 %conditional.1 = (f32[4,2,256]{2,1,0:T(2,128)S(1)}, f32[256,4,2,128]{0,3,2,1:T(8,128)S(1)}) conditional(s32[]{:T(128)} %convert_element_type.67, () %tuple.16, (s32[256]{0:T(256)S(1)}, s32[2048]{0:T(1024)S(1)}, s32[2048]{0:T(1024)S(1)}, bf16[256,8,128]{2,0,1:T(8,128)(2,1)S(1)}, bf16[2048,4,128]{2,0,1:T(8,128)(2,1)}, ...), branch_computations={%region_2.0_spmd, %region_3.5_spmd} | conditional | flops 2182610944 | bytes 51409964 | solution.py:106
  120.0 1.5 fusion.8
  121.5 6.6 %fusion = (f32[4,2,256]{2,1,0:T(2,128)S(1)}, f32[4,2048,256,2]{2,1,3,0:T(8,128)S(1)}) fusion(pred[256,2048]{0,1:T(8,128)(4,1)S(1)} %fusion.8, bf16[256,4,2,128]{3,0,2,1:T(8,128)(2,1)S(1)} %bitcast.92, bf16[2048,4,128]{2,0,1:T(8,128)(2,1)} %get-tuple-element.14), kind=kOutput, calls=%fused_computation.1 | convolution fusion | flops 1090516992 | bytes 19931136 | tf_op jit(solution)/shard_map/cond/branch_1_fun/qhrd,khd->hrqk/dot_general | solution.py:77
  128.1 5.7 %fusion.9 = f32[256,4,2,128]{3,0,2,1:T(8,128)S(1)} fusion(bf16[2048,4,128]{2,0,1:T(8,128)(2,1)S(1)} %copy-done.6, f32[4,2048,256,2]{2,1,3,0:T(8,128)S(1)} %get-tuple-element.31, pred[256,2048]{0,1:T(8,128)(4,1)S(1)} %fusion.8), kind=kOutput, calls=%fused_computation.10 | convolution fusion | flops 1090519040 | bytes 20447232 | tf_op jit(solution)/shard_map/cond/branch_1_fun/hrqk,khd->qhrd/dot_general | solution.py:86
  134.5 7.6 %convolution_convert_fusion = bf16[256,4608]{1,0:T(8,128)(2,1)} fusion(bf16[256,1024]{0,1:T(8,128)(2,1)S(1)} %bitcast.90, bf16[1024,4608]{1,0:T(8,128)(2,1)} %param.18), kind=kOutput, calls=%fused_computation.18 | convolution fusion | flops 2417098752 | bytes 12320768 | tf_op jit(solution)/shard_map/dot_general | solution.py:158
  142.3 95.0 %all-gather.12.cloned.1.call-done = bf16[1024,4608]{1,0:T(8,128)(2,1)} async-done(((bf16[256,4608]{1,0:T(8,128)(2,1)}), bf16[1024,4608]{1,0:T(8,128)(2,1)}) %all-gather.12.cloned.1.call-update) | async-done | bytes 9437200 | tf_op jit(solution)/shard_map/all_gather | solution.py:157
  237.3 6.5 %reduce_sum.58 = bf16[256,4608]{1,0:T(8,128)(2,1)S(1)} reduce(bf16[4,256,4608]{2,1,0:T(8,128)(2,1)} %bitcast.87, bf16[]{:T(256)} %constant.53.clone.1), dimensions={0}, to_apply=%region_5.6 | reduce | flops 3538944 | bytes 11796482 | tf_op jit(solution)/shard_map/reduce_sum | solution.py:156
  244.4 3.2 %fusion.19 = (f32[256]{0:T(256)S(1)}, bf16[256,4608]{1,0:T(8,128)(2,1)S(1)}) fusion(f32[4608]{0:T(1024)S(1)} %copy-done.5, f32[256]{0:T(256)S(1)} %add_rsqrt_fusion.1, bf16[256,4608]{1,0:T(8,128)(2,1)S(1)} %reduce_sum.58, bf16[256,4608]{1,0:T(8,128)(2,1)} %all-gather.6.cloned.1.call-done), kind=kLoop, calls=%fused_computation.25 | loop fusion | flops 10616576 | bytes 7098368 | tf_op jit(solution)/shard_map/reduce_sum | solution.py:21
  247.7 6.1 %convolution_bitcast_fusion = f32[32,8,8,128]{3,1,2,0:T(8,128)S(1)} fusion(bf16[4608,1024]{1,0:T(8,128)(2,1)} %param.21, bf16[256,4608]{1,0:T(8,128)(2,1)S(1)} %get-tuple-element.29, f32[4608]{0:T(1024)S(1)} %copy-done.8, f32[256]{0:T(256)S(1)} %add_rsqrt_fusion), kind=kOutput, calls=%fused_computation.37 | convolution fusion | flops 2420637696 | bytes 12864512 | tf_op jit(solution)/shard_map/dot_general | solution.py:46
  254.4 2.2 fusion.63
  256.6 1.2 reshape.224
  257.8 1.3 fusion.68
  259.1 4.5 %convolution_convert_fusion.1 = bf16[256,512]{1,0:T(8,128)(2,1)S(1)} fusion(bf16[4608,512]{1,0:T(8,128)(2,1)} %param.23, bf16[256,4608]{1,0:T(8,128)(2,1)} %copy-done.1, f32[4608]{0:T(1024)S(1)} %copy-done.8, f32[256]{0:T(256)S(1)} %add_rsqrt_fusion), kind=kOutput, calls=%fused_computation.40 | convolution fusion | flops 1212809216 | bytes 7359488 | tf_op jit(solution)/shard_map/dot_general | solution.py:52
  264.3 1.2 subtract_convert_fusion.2
  265.6 0.7 pad_maximum_fusion.2
  266.4 4.1 %collective-permute-start = (bf16[2,128,4,128]{3,1,2,0:T(8,128)(2,1)}, bf16[2,128,4,128]{3,1,2,0:T(8,128)(2,1)}, u32[]{:S(2)}, u32[]{:S(2)}) collective-permute-start(bf16[2,128,4,128]{3,1,2,0:T(8,128)(2,1)} %pad_maximum_fusion.2), channel_id=1, source_target_pairs={{0,4},{4,8},{8,12},{12,16},{16,20},{20,24},{24,28},{1,5},{5,9},{9,... | collective-permute-start | bytes 786440 | tf_op jit(solution)/shard_map/ppermute | solution.py:16
  270.4 1.4 subtract_convert_fusion
  272.0 1.9 constant_dynamic-slice_fusion
  273.9 1.0 slice_bitcast_fusion.1
  275.0 2.6 fusion.26
  277.6 1.1 divide_convert_fusion
  278.7 1.0 copy.43
  (61 shorter events, 6.7 us)
Async XLA Ops:
  7.2 41.9 %all-gather.6.cloned.1.call-start = ((), (), s32[]{:S(2)}) async-start(), calls=%async_computation | async-start | bytes 2949120 | tf_op jit(solution)/shard_map/all_gather | solution.py:150
  7.9 81.3 %all-gather.8.cloned.1.call-start = ((), (), s32[]{:S(2)}) async-start(), calls=%async_computation.1 | async-start | bytes 2359296 | tf_op jit(solution)/shard_map/all_gather | solution.py:114
  56.6 2.8 copy-start
  56.6 2.8 copy-start.7
  59.3 60.7 %all-gather.10.cloned.1.call-start = ((), (), s32[]{:S(2)}) async-start(), calls=%async_computation.2 | async-start | bytes 2359296 | tf_op jit(solution)/shard_map/all_gather | solution.py:115
  64.0 173.4 %all-gather.12.cloned.1.call-start = ((), (), s32[]{:S(2)}) async-start(), calls=%async_computation.3 | async-start | bytes 11796480 | tf_op jit(solution)/shard_map/all_gather | solution.py:157
  121.5 6.6 %copy-start.6 = (bf16[2048,4,128]{2,0,1:T(8,128)(2,1)S(1)}, bf16[2048,4,128]{2,0,1:T(8,128)(2,1)}, u32[]{:S(2)}) copy-start(bf16[2048,4,128]{2,0,1:T(8,128)(2,1)} %get-tuple-element.16) | copy-start | bytes 6291460 | tf_op jit(solution)/shard_map/cond
  237.3 7.1 %copy-start.5 = (f32[4608]{0:T(1024)S(1)}, f32[4608]{0:T(1024)}, u32[]{:S(2)}) copy-start(f32[4608]{0:T(1024)} %param.19) | copy-start | bytes 55300
  243.8 3.8 %copy-start.8 = (f32[4608]{0:T(1024)S(1)}, f32[4608]{0:T(1024)}, u32[]{:S(2)}) copy-start(f32[4608]{0:T(1024)} %param.20) | copy-start | bytes 55300
  244.4 10.0 %slice-start = ((s8[4718592]{0:T(1024)(128)(4,1)}), s8[4194304]{0:T(1024)(128)(4,1)S(1)}, s32[]{:S(2)}) async-start(s8[4718592]{0:T(1024)(128)(4,1)} %bitcast.98), calls=%async_computation.4 | async-start | bytes 8388608
  247.6 6.7 %copy-start.1 = (bf16[256,4608]{1,0:T(8,128)(2,1)}, bf16[256,4608]{1,0:T(8,128)(2,1)S(1)}, u32[]{:S(2)}) copy-start(bf16[256,4608]{1,0:T(8,128)(2,1)S(1)} %get-tuple-element.29) | copy-start | bytes 7077892
  247.7 6.7 %slice-start.1 = ((s8[4718592]{0:T(1024)(128)(4,1)}), s8[524288]{0:T(1024)(128)(4,1)S(1)}, s32[]{:S(2)}) async-start(s8[4718592]{0:T(1024)(128)(4,1)} %bitcast.98), calls=%async_computation.5 | async-start | bytes 1048576
  259.1 5.2 %copy-start.2 = (f32[256,4,64]{2,1,0:T(4,128)S(1)}, f32[256,4,64]{2,1,0:T(4,128)}, u32[]{:S(2)}) copy-start(f32[256,4,64]{2,1,0:T(4,128)} %get-tuple-element.44) | copy-start | bytes 786436
  263.6 0.7 copy-start.3
  265.5 6.3 %copy-start.4 = (bf16[256,512]{1,0:T(8,128)(2,1)S(1)}, bf16[256,512]{1,0:T(8,128)(2,1)}, u32[]{:S(2)}) copy-start(bf16[256,512]{1,0:T(8,128)(2,1)} %copy-done.3) | copy-start | bytes 786436
  266.4 7.5 %collective-permute-start = (bf16[2,128,4,128]{3,1,2,0:T(8,128)(2,1)}, bf16[2,128,4,128]{3,1,2,0:T(8,128)(2,1)}, u32[]{:S(2)}, u32[]{:S(2)}) collective-permute-start(bf16[2,128,4,128]{3,1,2,0:T(8,128)(2,1)} %pad_maximum_fusion.2), channel_id=1, source_target_pairs={{0,4},{4,8},{8,12},{12,16},{16,20},{20,24},{24,28},{1,5},{5,9},{9,... | collective-permute-start | bytes 786440 | tf_op jit(solution)/shard_map/ppermute | solution.py:16
Sparse Core Ops, SparseCore 0:
  9.8 39.2 all-gather.5
  59.5 29.7 all-gather.7
  91.4 28.5 all-gather.9
  142.2 95.0 all-gather.11
